TPU v7x, 32 devices: a whole 2x2x4 slice. The times are simulated.
32 devices in a mesh: io: 16 (over z, x, core), rep: 2 (over y).
Axes of the slice: x: 2, y: 2, z: 4, core: 2. Of those that a mesh axis runs over, the one named last changes fastest.
Arguments:
- snapshots: float32 [49152, 2048], P(('rep', 'io')), parts along dimension 0, may hold values from -6 to 6
Outputs:
- coefficients: float32 [32, 256, 2048], P('rep', None, 'io'), parts along dimension 0
- resid_var: float32 [512, 2048], P('rep', 'io'), parts along dimension 0
There are 2 independent parts, one for each index of `rep`. A program takes and returns all parts, laid end to end along the dimension named above; each array names one. Nothing has to cross between parts.
All inputs are finite; a program needn't handle non-finite values.
Results may differ from a plain program's by a relative error of at most 0.000071.
Values sent between devices are 32-bit elements; how exact they have to be, the bound alone decides.
A program may use at most 128 MiB of HBM per device.

v0:
```python
import functools

import jax
import jax.numpy as jnp
import numpy as np
from jax import lax
from jax.experimental import pallas as pl
from jax.experimental.pallas import tpu as pltpu
from jax.sharding import PartitionSpec as P

TIMES = 96
HARM = 16
MONTHS = 12
SPAN = 24
CHAIN = TIMES // SPAN
SLOW = 4
SUMS = MONTHS + SLOW + 1
LANES = 128
ROWS = 8
AHEAD = 8
CLOSE_LAG = 3
MESH = pl.DeviceIdType.MESH


def fit_constants():
    steps = np.arange(TIMES, dtype=np.float64)
    slow = np.stack(
        [
            (steps - (TIMES - 1) / 2.0) / (TIMES / 2.0),
            np.cos(2.0 * np.pi * steps / TIMES),
            np.sin(2.0 * np.pi * steps / TIMES),
            np.cos(4.0 * np.pi * steps / TIMES),
        ],
        axis=1,
    )
    month = np.arange(MONTHS, dtype=np.float64)
    angles = 2.0 * np.pi * month / MONTHS
    periodic = [np.cos(j * angles) for j in range(7)] + [np.sin(j * angles) for j in range(1, 6)]
    unmix = np.linalg.inv(np.stack(periodic, axis=1))
    years = TIMES // MONTHS
    cross = slow.reshape(years, MONTHS, SLOW).sum(axis=0)
    inner = np.linalg.inv(slow.T @ slow - cross.T @ cross / years)
    return slow, cross, inner, unmix, years


def dot(weights, values):
    total = None
    for weight, value in zip(weights, values):
        term = value * np.float32(weight)
        total = term if total is None else total + term
    return total


def finish(sums):
    _, cross, inner, unmix, years = fit_constants()
    by_month, moments, squares = sums[:MONTHS], sums[MONTHS : MONTHS + SLOW], sums[-1]
    reduced = [moments[k] - dot(cross[:, k] / years, by_month) for k in range(SLOW)]
    slow = [dot(inner[k], reduced) for k in range(SLOW)]
    level = [(by_month[m] - dot(cross[m], slow)) * np.float32(1.0 / years) for m in range(MONTHS)]
    explained = slow[0] * moments[0]
    for k in range(1, SLOW):
        explained = explained + slow[k] * moments[k]
    for m in range(MONTHS):
        explained = explained + level[m] * by_month[m]
    half = MONTHS // 2
    even = [level[0]] + [level[m] + level[MONTHS - m] for m in range(1, half)] + [level[half]]
    odd = [level[m] - level[MONTHS - m] for m in range(1, half)]
    cosines = [dot(unmix[j, : half + 1], even) for j in range(half + 1)]
    sines = [dot(unmix[half + j, 1:half], odd) for j in range(1, half)]
    coeffs = [cosines[0], slow[0]] + cosines[1:] + sines + slow[1:]
    return coeffs, (squares - explained) * np.float32(1.0 / TIMES)


def kernel(
    groups, lat, local_rows,
    field, coeff_out, var_out,
    raw, part, below, above,
    raw_send, raw_recv, part_send, below_recv, above_recv,
):
    members = groups // CHAIN
    chunks = lat // ROWS
    me = lax.axis_index("io")
    link, member = me // members, lax.rem(me, members)
    device = lambda at, who: {"io": at * members + who}

    span = fit_constants()[0][:SPAN]
    offset = link.astype(jnp.float32) * np.float32(SPAN / (TIMES / 2.0))
    quarter = lambda at: (link == at).astype(jnp.float32)
    turn_cos, turn_sin = quarter(0) - quarter(2), quarter(1) - quarter(3)
    flip = quarter(0) - quarter(1) + quarter(2) - quarter(3)

    barrier = pltpu.get_barrier_semaphore()
    for step in range(1, members):
        other = lax.rem(member + step, members)
        pl.semaphore_signal(barrier, inc=1, device_id=device(link, other), device_id_type=MESH)

    @pl.when(link > 0)
    def _():
        pl.semaphore_signal(barrier, inc=1, device_id=device(link - 1, member), device_id_type=MESH)

    @pl.when(link < CHAIN - 1)
    def _():
        pl.semaphore_signal(barrier, inc=1, device_id=device(link + 1, member), device_id_type=MESH)

    ends = (link == 0).astype(jnp.int32) + (link == CHAIN - 1).astype(jnp.int32)
    pl.semaphore_wait(barrier, members + 1 - ends)

    def block_at(rank):
        orders = []
        for at in range(CHAIN):
            up, down = list(range(CHAIN - 1, at, -1)), list(range(at))
            orders.append((up + down if len(up) >= len(down) else down + up) + [at])
        return sum((link == at).astype(jnp.int32) * orders[at][rank] for at in range(CHAIN))

    def spread_rows(chunk, to, row, count, time):
        for step in list(range(1, members)) + [0]:
            other = lax.rem(member + step, members)
            lon = pl.multiple_of((to * members + other) * LANES, LANES)
            if count is None:
                src = field.at[pl.ds(row, ROWS), pl.ds(lon, LANES)]
                dst = raw.at[chunk, to, time]
            else:
                src = field.at[:, pl.ds(row, ROWS), pl.ds(lon, LANES)]
                dst = raw.at[chunk, to, pl.ds(time, count)]
            if step == 0:
                pltpu.make_async_copy(src, dst, raw_recv.at[chunk, to]).start()
            else:
                pltpu.make_async_remote_copy(
                    src_ref=src, dst_ref=dst, send_sem=raw_send, recv_sem=raw_recv.at[chunk, to],
                    device_id=device(link, other), device_id_type=MESH,
                ).start()

    def spread_block(chunk, to):
        if local_rows % lat == 0:
            count = local_rows // lat
            spread_rows(chunk, to, pl.multiple_of(chunk * ROWS, ROWS), count, member * count)
        else:
            first = member * local_rows
            for extra in range(local_rows // lat + 2):
                time = first // lat + extra
                row = time * lat + chunk * ROWS - first

                @pl.when((row >= 0) & (row < local_rows))
                def _():
                    spread_rows(chunk, to, pl.multiple_of(row, ROWS), None, time)

    def each(step, act):
        for rank in range(CHAIN):

            @pl.when((step >= rank) & (step < chunks + rank))
            def _():
                act(step - rank, block_at(rank))

    def send(chunk, to, up):
        pltpu.make_async_remote_copy(
            src_ref=part.at[chunk, to],
            dst_ref=(below if up else above).at[chunk, to],
            send_sem=part_send,
            recv_sem=(below_recv if up else above_recv).at[chunk, to],
            device_id=device(link + 1 if up else link - 1, member),
            device_id_type=MESH,
        ).start()

    def arrive(chunk, to, up):
        box, sem = (below, below_recv) if up else (above, above_recv)
        pltpu.make_async_copy(box.at[chunk, to], box.at[chunk, to], sem.at[chunk, to]).wait()
        for k in range(SUMS):
            part[chunk, to, k] = part[chunk, to, k] + box[chunk, to, k]

    def add_up(chunk, to):
        pltpu.make_async_copy(raw.at[chunk, to], raw.at[chunk, to], raw_recv.at[chunk, to]).wait()
        local = [None] * (SLOW + 1)
        whole = None
        for month in range(MONTHS):
            kept = None
            for time in range(month, SPAN, MONTHS):
                value = raw[chunk, to, time]
                kept = value if kept is None else kept + value
                terms = [value * np.float32(span[time, k]) for k in range(SLOW)] + [value * value]
                local = [term if own is None else own + term for own, term in zip(local, terms)]
            part[chunk, to, month] = kept
            whole = kept if whole is None else whole + kept
        trend, cosine, sine, double, squares = local
        part[chunk, to, MONTHS] = trend + whole * offset
        part[chunk, to, MONTHS + 1] = cosine * turn_cos - sine * turn_sin
        part[chunk, to, MONTHS + 2] = cosine * turn_sin + sine * turn_cos
        part[chunk, to, MONTHS + 3] = double * flip
        part[chunk, to, MONTHS + 4] = squares

        @pl.when((link == 0) & (to > 0))
        def _():
            send(chunk, to, True)

        @pl.when((link == CHAIN - 1) & (to < CHAIN - 1))
        def _():
            send(chunk, to, False)

    def relay(step):
        for at in range(1, CHAIN - 1):
            for to in range(CHAIN - 1, at, -1):
                lag = CHAIN - 1 - to + at

                @pl.when((link == at) & (step >= lag) & (step < chunks + lag))
                def _():
                    arrive(step - lag, to, True)
                    send(step - lag, to, True)

            for to in range(at):
                lag = to + CHAIN - 1 - at

                @pl.when((link == at) & (step >= lag) & (step < chunks + lag))
                def _():
                    arrive(step - lag, to, False)
                    send(step - lag, to, False)

    def close(chunk):
        @pl.when(link > 0)
        def _():
            arrive(chunk, link, True)

        @pl.when(link < CHAIN - 1)
        def _():
            arrive(chunk, link, False)

        coeffs, variance = finish([part[chunk, link, k] for k in range(SUMS)])
        rows = pl.ds(pl.multiple_of(chunk * ROWS, ROWS), ROWS)
        for k in range(HARM):
            coeff_out[k, rows, :] = coeffs[k]
        var_out[rows, :] = variance

    ramp = CHAIN - 1
    lax.fori_loop(0, AHEAD, lambda step, _: (each(step, spread_block), 0)[1], 0)

    def body(step, carry):
        each(step + AHEAD, spread_block)
        each(step, add_up)
        relay(step)

        @pl.when(step >= ramp + CLOSE_LAG)
        def _():
            close(step - ramp - CLOSE_LAG)

        return carry

    lax.fori_loop(0, chunks + ramp + CLOSE_LAG, body, 0)

    lons = pl.ds(0, (members - 1) * CHAIN * LANES)
    sent = field.at[:, :, lons] if local_rows % lat == 0 else field.at[:, lons]
    pltpu.make_async_copy(sent, sent, raw_send).wait()
    passed = part.at[:, pl.ds(0, CHAIN - 1)]
    pltpu.make_async_copy(passed, passed, part_send).wait()


def put_out(coeffs, variance, coeff_out, var_out, sem):
    copies = [
        pltpu.make_async_copy(coeffs, coeff_out, sem.at[0]),
        pltpu.make_async_copy(variance, var_out, sem.at[1]),
    ]
    for copy in copies:
        copy.start()
    for copy in copies:
        copy.wait()


def local(snapshots):
    groups = lax.axis_size("io")
    local_rows, width = snapshots.shape
    lat = local_rows * groups // TIMES
    if width != groups * LANES or lat % ROWS or local_rows % ROWS or groups % CHAIN:
        raise ValueError("unsupported sizes")
    chunks = lat // ROWS
    field = snapshots.reshape(local_rows // lat, lat, width) if local_rows % lat == 0 else snapshots
    results = pl.pallas_call(
        functools.partial(kernel, groups, lat, local_rows),
        out_shape=(
            jax.ShapeDtypeStruct((HARM, lat, LANES), jnp.float32),
            jax.ShapeDtypeStruct((lat, LANES), jnp.float32),
        ),
        in_specs=[pl.BlockSpec(memory_space=pl.ANY)],
        out_specs=(pl.BlockSpec(memory_space=pltpu.VMEM), pl.BlockSpec(memory_space=pltpu.VMEM)),
        scratch_shapes=[
            pltpu.VMEM((chunks, CHAIN, SPAN, ROWS, LANES), jnp.float32),
            pltpu.VMEM((chunks, CHAIN, SUMS, ROWS, LANES), jnp.float32),
            pltpu.VMEM((chunks, CHAIN, SUMS, ROWS, LANES), jnp.float32),
            pltpu.VMEM((chunks, CHAIN, SUMS, ROWS, LANES), jnp.float32),
            pltpu.SemaphoreType.DMA,
            pltpu.SemaphoreType.DMA((chunks, CHAIN)),
            pltpu.SemaphoreType.DMA,
            pltpu.SemaphoreType.DMA((chunks, CHAIN)),
            pltpu.SemaphoreType.DMA((chunks, CHAIN)),
        ],
        compiler_params=pltpu.CompilerParams(
            collective_id=0, has_side_effects=True, vmem_limit_bytes=44 * 2**20
        ),
        name="climatology",
    )(field)
    return pl.pallas_call(
        put_out,
        out_shape=tuple(jax.ShapeDtypeStruct(r.shape, r.dtype) for r in results),
        in_specs=[pl.BlockSpec(memory_space=pltpu.VMEM)] * 2,
        out_specs=(pl.BlockSpec(memory_space=pl.ANY),) * 2,
        scratch_shapes=[pltpu.SemaphoreType.DMA((2,))],
        compiler_params=pltpu.CompilerParams(vmem_limit_bytes=4 * 2**20),
        name="put_out",
    )(*results)


def solution(mesh):
    return jax.shard_map(
        local,
        mesh=mesh,
        in_specs=(P(("rep", "io"), None),),
        out_specs=(P("rep", None, "io"), P("rep", "io")),
        check_vma=False,
    )
```

profile of v0, /device:TPU:17, one launch (start us, length us, event | category | flops | bytes accessed | tf_op | source)
XLA Modules:
  0.0 156.5 jit_solution(12042988322865266141)
XLA Ops:
  0.6 154.5 %climatology.1 = (f32[16,256,128]{2,1,0:T(8,128)S(1)}, f32[256,128]{1,0:T(8,128)S(1)}) custom-call(f32[6,256,2048]{2,1,0:T(8,128)} %bitcast.1), custom_call_target="tpu_custom_call" | custom-call | tf_op jit(solution)/shard_map/climatology/pallas_call | solution.py:273
  155.1 1.4 put_out.1
where the time goes:
time: 159 us; the launch traced here: 156 us
  Pallas kernels  156 us (98%)
    pallas_call x1, Pallas kernels, local(): pl.pallas_call(functools.partial(kernel, groups, lat, local_rows), out_sh...  154 us

commit v1 on v0

--- a/solution.py
+++ b/solution.py
@@ -17,9 +17,41 @@
 SUMS = MONTHS + SLOW + 1
 LANES = 128
 ROWS = 8
-AHEAD = 8
-CLOSE_LAG = 3
+AHEAD = 4
+SKEW = 3
 MESH = pl.DeviceIdType.MESH
+
+
+def schedule():
+    far = [[to for to in sorted(range(CHAIN), key=lambda to: -abs(to - at)) if to != at] for at in range(CHAIN)]
+    orders = [blocks + [at] for at, blocks in enumerate(far)]
+    added = []
+    for at in range(CHAIN):
+        lags, near = {}, min(at, CHAIN - 1 - at)
+        for to in far[at]:
+            side = [other for other in far[at] if (other > at) == (to > at)]
+            lags[to] = SKEW * side.index(to)
+        lags[at] = SKEW * (CHAIN - 2)
+        added.append(lags)
+    up, down = {}, {}
+    for to in range(CHAIN):
+        for at in range(to + 1):
+            up[at, to] = added[0][to] if at == 0 else max(added[at][to], up[at - 1, to] + 1)
+        for at in range(CHAIN - 1, to - 1, -1):
+            down[at, to] = added[at][to] if at == CHAIN - 1 else max(added[at][to], down[at + 1, to] + 1)
+    hold = max(
+        [up[at + 1, to] - up[at, to] for at, to in up if at < to]
+        + [down[at - 1, to] - down[at, to] for at, to in down if at > to]
+    )
+    close = [max(up[at, at], down[at, at]) for at in range(CHAIN)]
+    last = max([lag for (at, to), lag in up.items() if at < to] + [lag for (at, to), lag in down.items() if at > to])
+    return orders, added, up, down, close, hold, last
+
+
+ORDERS, ADDED, UP, DOWN, CLOSE, HOLD, LAST_SENT = schedule()
+LAST_ADDED = max(max(lags.values()) for lags in ADDED)
+RAW_SLOTS = AHEAD + 2
+BOX_SLOTS = HOLD + 4
 
 
 def fit_constants():
@@ -75,7 +107,7 @@
     groups, lat, local_rows,
     field, coeff_out, var_out,
     raw, part, below, above,
-    raw_send, raw_recv, part_send, below_recv, above_recv,
+    raw_send, raw_recv, part_send, box_recv, member_free, box_free,
 ):
     members = groups // CHAIN
     chunks = lat // ROWS
@@ -89,6 +121,9 @@
     turn_cos, turn_sin = quarter(0) - quarter(2), quarter(1) - quarter(3)
     flip = quarter(0) - quarter(1) + quarter(2) - quarter(3)
 
+    def by_link(values):
+        return sum((link == at).astype(jnp.int32) * values[at] for at in range(CHAIN))
+
     barrier = pltpu.get_barrier_semaphore()
     for step in range(1, members):
         other = lax.rem(member + step, members)
@@ -104,13 +139,6 @@
 
     ends = (link == 0).astype(jnp.int32) + (link == CHAIN - 1).astype(jnp.int32)
     pl.semaphore_wait(barrier, members + 1 - ends)
-
-    def block_at(rank):
-        orders = []
-        for at in range(CHAIN):
-            up, down = list(range(CHAIN - 1, at, -1)), list(range(at))
-            orders.append((up + down if len(up) >= len(down) else down + up) + [at])
-        return sum((link == at).astype(jnp.int32) * orders[at][rank] for at in range(CHAIN))
 
     def spread_rows(chunk, to, row, count, time):
         for step in list(range(1, members)) + [0]:
@@ -122,11 +150,12 @@
             else:
                 src = field.at[:, pl.ds(row, ROWS), pl.ds(lon, LANES)]
                 dst = raw.at[chunk, to, pl.ds(time, count)]
+            arrived = raw_recv.at[lax.rem(chunk, RAW_SLOTS), to]
             if step == 0:
-                pltpu.make_async_copy(src, dst, raw_recv.at[chunk, to]).start()
+                pltpu.make_async_copy(src, dst, arrived).start()
             else:
                 pltpu.make_async_remote_copy(
-                    src_ref=src, dst_ref=dst, send_sem=raw_send, recv_sem=raw_recv.at[chunk, to],
+                    src_ref=src, dst_ref=dst, send_sem=raw_send, recv_sem=arrived,
                     device_id=device(link, other), device_id_type=MESH,
                 ).start()
 
@@ -146,29 +175,75 @@
 
     def each(step, act):
         for rank in range(CHAIN):
-
-            @pl.when((step >= rank) & (step < chunks + rank))
+            lag = by_link([ADDED[at][ORDERS[at][rank]] for at in range(CHAIN)])
+
+            @pl.when((step >= lag) & (step < chunks + lag))
             def _():
-                act(step - rank, block_at(rank))
+                act(step - lag, by_link([ORDERS[at][rank] for at in range(CHAIN)]))
+
+    spread_steps = chunks + LAST_ADDED
+
+    def spread(step):
+        @pl.when((step >= RAW_SLOTS) & (step < spread_steps))
+        def _():
+            for away in range(1, members):
+                pl.semaphore_wait(member_free.at[away], 1)
+
+        each(step, spread_block)
+
+    def free_members(step):
+        @pl.when(step + RAW_SLOTS < spread_steps)
+        def _():
+            for away in range(1, members):
+                other = lax.rem(member + away, members)
+                pl.semaphore_signal(
+                    member_free.at[members - away], inc=1, device_id=device(link, other), device_id_type=MESH
+                )
+
+    send_steps, slack = chunks + LAST_SENT, BOX_SLOTS - HOLD
+
+    def await_boxes(step):
+        for up in (True, False):
+
+            @pl.when((link < CHAIN - 1 if up else link > 0) & (step >= slack) & (step < send_steps))
+            def _():
+                pl.semaphore_wait(box_free.at[0 if up else 1], 1)
+
+    def free_boxes(step):
+        for up in (True, False):
+
+            @pl.when((link > 0 if up else link < CHAIN - 1) & (step + slack < send_steps))
+            def _():
+                pl.semaphore_signal(
+                    box_free.at[0 if up else 1], inc=1,
+                    device_id=device(link - 1 if up else link + 1, member), device_id_type=MESH,
+                )
+
+    def box_sem(chunk, to, up, at):
+        where = to if up else to + (to == at).astype(jnp.int32) * (CHAIN - to)
+        return box_recv.at[lax.rem(chunk, BOX_SLOTS), where]
 
     def send(chunk, to, up):
+        at = link + 1 if up else link - 1
         pltpu.make_async_remote_copy(
             src_ref=part.at[chunk, to],
             dst_ref=(below if up else above).at[chunk, to],
             send_sem=part_send,
-            recv_sem=(below_recv if up else above_recv).at[chunk, to],
-            device_id=device(link + 1 if up else link - 1, member),
+            recv_sem=box_sem(chunk, to, up, at),
+            device_id=device(at, member),
             device_id_type=MESH,
         ).start()
 
     def arrive(chunk, to, up):
-        box, sem = (below, below_recv) if up else (above, above_recv)
-        pltpu.make_async_copy(box.at[chunk, to], box.at[chunk, to], sem.at[chunk, to]).wait()
+        box = below if up else above
+        pltpu.make_async_copy(box.at[chunk, to], box.at[chunk, to], box_sem(chunk, to, up, link)).wait()
         for k in range(SUMS):
             part[chunk, to, k] = part[chunk, to, k] + box[chunk, to, k]
 
     def add_up(chunk, to):
-        pltpu.make_async_copy(raw.at[chunk, to], raw.at[chunk, to], raw_recv.at[chunk, to]).wait()
+        pltpu.make_async_copy(
+            raw.at[chunk, to], raw.at[chunk, to], raw_recv.at[lax.rem(chunk, RAW_SLOTS), to]
+        ).wait()
         local = [None] * (SLOW + 1)
         whole = None
         for month in range(MONTHS):
@@ -197,21 +272,16 @@
 
     def relay(step):
         for at in range(1, CHAIN - 1):
-            for to in range(CHAIN - 1, at, -1):
-                lag = CHAIN - 1 - to + at
+            for to in range(CHAIN):
+                if to == at:
+                    continue
+                lag = UP[at, to] if to > at else DOWN[at, to]
 
                 @pl.when((link == at) & (step >= lag) & (step < chunks + lag))
                 def _():
-                    arrive(step - lag, to, True)
-                    send(step - lag, to, True)
-
-            for to in range(at):
-                lag = to + CHAIN - 1 - at
-
-                @pl.when((link == at) & (step >= lag) & (step < chunks + lag))
-                def _():
-                    arrive(step - lag, to, False)
-                    send(step - lag, to, False)
+                    where = jnp.int32(to)
+                    arrive(step - lag, where, to > at)
+                    send(step - lag, where, to > at)
 
     def close(chunk):
         @pl.when(link > 0)
@@ -228,21 +298,24 @@
             coeff_out[k, rows, :] = coeffs[k]
         var_out[rows, :] = variance
 
-    ramp = CHAIN - 1
-    lax.fori_loop(0, AHEAD, lambda step, _: (each(step, spread_block), 0)[1], 0)
+    lax.fori_loop(0, AHEAD, lambda step, _: (spread(step), 0)[1], 0)
+    close_lag = by_link(CLOSE)
 
     def body(step, carry):
-        each(step + AHEAD, spread_block)
+        spread(step + AHEAD)
+        await_boxes(step)
         each(step, add_up)
+        free_members(step)
         relay(step)
 
-        @pl.when(step >= ramp + CLOSE_LAG)
-        def _():
-            close(step - ramp - CLOSE_LAG)
-
+        @pl.when((step >= close_lag) & (step < chunks + close_lag))
+        def _():
+            close(step - close_lag)
+
+        free_boxes(step)
         return carry
 
-    lax.fori_loop(0, chunks + ramp + CLOSE_LAG, body, 0)
+    lax.fori_loop(0, chunks + max(max(CLOSE), LAST_SENT), body, 0)
 
     lons = pl.ds(0, (members - 1) * CHAIN * LANES)
     sent = field.at[:, :, lons] if local_rows % lat == 0 else field.at[:, lons]
@@ -269,6 +342,7 @@
     if width != groups * LANES or lat % ROWS or local_rows % ROWS or groups % CHAIN:
         raise ValueError("unsupported sizes")
     chunks = lat // ROWS
+    members = groups // CHAIN
     field = snapshots.reshape(local_rows // lat, lat, width) if local_rows % lat == 0 else snapshots
     results = pl.pallas_call(
         functools.partial(kernel, groups, lat, local_rows),
@@ -284,10 +358,11 @@
             pltpu.VMEM((chunks, CHAIN, SUMS, ROWS, LANES), jnp.float32),
             pltpu.VMEM((chunks, CHAIN, SUMS, ROWS, LANES), jnp.float32),
             pltpu.SemaphoreType.DMA,
-            pltpu.SemaphoreType.DMA((chunks, CHAIN)),
+            pltpu.SemaphoreType.DMA((RAW_SLOTS, CHAIN)),
             pltpu.SemaphoreType.DMA,
-            pltpu.SemaphoreType.DMA((chunks, CHAIN)),
-            pltpu.SemaphoreType.DMA((chunks, CHAIN)),
+            pltpu.SemaphoreType.DMA((BOX_SLOTS, CHAIN + 1)),
+            pltpu.SemaphoreType.REGULAR((members,)),
+            pltpu.SemaphoreType.REGULAR((2,)),
         ],
         compiler_params=pltpu.CompilerParams(
             collective_id=0, has_side_effects=True, vmem_limit_bytes=44 * 2**20

time: 159 us -> 154 us (0.969); the launches traced: 156 us -> 154 us
  Pallas kernels: 156 us -> 153 us
    pallas_call x1, Pallas kernels: 154 us -> 152 us  [local(): pl.pallas_call(functools.partial(kernel, groups, lat, local_rows), out_sh...]
where the time goes in v1:
time: 154 us
  Pallas kernels  153 us (99%)
    pallas_call x1, Pallas kernels, local(): pl.pallas_call(functools.partial(kernel, groups, lat, local_rows), out_sh...  152 us

profile of v1, /device:TPU:17, one launch (start us, length us, event | category | flops | bytes accessed | tf_op | source)
XLA Modules:
  0.0 153.7 jit_solution(10321926083952714076)
XLA Ops:
  0.6 151.7 %climatology.1 = (f32[16,256,128]{2,1,0:T(8,128)S(1)}, f32[256,128]{1,0:T(8,128)S(1)}) custom-call(f32[6,256,2048]{2,1,0:T(8,128)} %bitcast.1), custom_call_target="tpu_custom_call" | custom-call | tf_op jit(solution)/shard_map/climatology/pallas_call | solution.py:347
  152.3 1.4 put_out.1

commit v2 on v1

--- a/solution.py
+++ b/solution.py
@@ -19,6 +19,9 @@
 ROWS = 8
 AHEAD = 4
 SKEW = 3
+EARLY_EVEN, EARLY_ODD = 2, 1
+EARLY = max(EARLY_EVEN, EARLY_ODD)
+FORWARD = 2
 MESH = pl.DeviceIdType.MESH
 
 
@@ -27,11 +30,11 @@
     orders = [blocks + [at] for at, blocks in enumerate(far)]
     added = []
     for at in range(CHAIN):
-        lags, near = {}, min(at, CHAIN - 1 - at)
+        lags = {}
         for to in far[at]:
             side = [other for other in far[at] if (other > at) == (to > at)]
             lags[to] = SKEW * side.index(to)
-        lags[at] = SKEW * (CHAIN - 2)
+        lags[at] = SKEW + 1 if at in (0, CHAIN - 1) else SKEW * (CHAIN - 2)
         added.append(lags)
     up, down = {}, {}
     for to in range(CHAIN):
@@ -39,11 +42,13 @@
             up[at, to] = added[0][to] if at == 0 else max(added[at][to], up[at - 1, to] + 1)
         for at in range(CHAIN - 1, to - 1, -1):
             down[at, to] = added[at][to] if at == CHAIN - 1 else max(added[at][to], down[at + 1, to] + 1)
+    close = [max(up[at, at], down[at, at]) for at in range(CHAIN)]
+    for at in range(CHAIN):
+        up[at, at] = down[at, at] = close[at]
     hold = max(
         [up[at + 1, to] - up[at, to] for at, to in up if at < to]
         + [down[at - 1, to] - down[at, to] for at, to in down if at > to]
     )
-    close = [max(up[at, at], down[at, at]) for at in range(CHAIN)]
     last = max([lag for (at, to), lag in up.items() if at < to] + [lag for (at, to), lag in down.items() if at > to])
     return orders, added, up, down, close, hold, last
 
@@ -51,7 +56,7 @@
 ORDERS, ADDED, UP, DOWN, CLOSE, HOLD, LAST_SENT = schedule()
 LAST_ADDED = max(max(lags.values()) for lags in ADDED)
 RAW_SLOTS = AHEAD + 2
-BOX_SLOTS = HOLD + 4
+BOX_SLOTS = HOLD + 3
 
 
 def fit_constants():
@@ -108,21 +113,39 @@
     field, coeff_out, var_out,
     raw, part, below, above,
     raw_send, raw_recv, part_send, box_recv, member_free, box_free,
+    *direct,
 ):
     members = groups // CHAIN
     chunks = lat // ROWS
+    held = local_rows // lat
+    early = EARLY if direct else 0
+    if direct:
+        stage, first_stage, passing, early_raw, stage_sem, passing_recv, early_recv, early_send = direct
     me = lax.axis_index("io")
     link, member = me // members, lax.rem(me, members)
     device = lambda at, who: {"io": at * members + who}
 
     span = fit_constants()[0][:SPAN]
-    offset = link.astype(jnp.float32) * np.float32(SPAN / (TIMES / 2.0))
-    quarter = lambda at: (link == at).astype(jnp.float32)
-    turn_cos, turn_sin = quarter(0) - quarter(2), quarter(1) - quarter(3)
-    flip = quarter(0) - quarter(1) + quarter(2) - quarter(3)
-
+    at_end = (link == 0) | (link == CHAIN - 1)
+    early_of = lambda who: EARLY_ODD + (EARLY_EVEN - EARLY_ODD) * (1 - lax.rem(who, 2))
+    own_early = early_of(member)
     def by_link(values):
         return sum((link == at).astype(jnp.int32) * values[at] for at in range(CHAIN))
+
+    inner = by_link([1, 0, CHAIN - 1, CHAIN - 2])
+
+    def block_of(chunk, to):
+        lons = pl.ds(pl.multiple_of(to * members * LANES, LANES), members * LANES)
+        return field.at[:, pl.ds(chunk * ROWS, ROWS), lons]
+
+    first_to = by_link([ORDERS[at][0] for at in range(CHAIN)])
+    if direct:
+        pltpu.make_async_copy(block_of(0, first_to), first_stage, stage_sem.at[0]).start()
+
+        @pl.when(at_end)
+        def _():
+            for chunk in range(early):
+                pltpu.make_async_copy(block_of(chunk, inner), stage.at[chunk], stage_sem.at[1 + chunk]).start()
 
     barrier = pltpu.get_barrier_semaphore()
     for step in range(1, members):
@@ -140,24 +163,30 @@
     ends = (link == 0).astype(jnp.int32) + (link == CHAIN - 1).astype(jnp.int32)
     pl.semaphore_wait(barrier, members + 1 - ends)
 
-    def spread_rows(chunk, to, row, count, time):
+    def spread_one(chunk, to, step, row, count=held, time=None, staged=None):
+        other = lax.rem(member + step, members)
+        time = member * held if time is None else time
+        lon = pl.multiple_of((to * members + other) * LANES, LANES)
+        if count is None:
+            src = field.at[pl.ds(row, ROWS), pl.ds(lon, LANES)]
+            dst = raw.at[chunk, to, time]
+        else:
+            src = field.at[:, pl.ds(row, ROWS), pl.ds(lon, LANES)]
+            if staged is not None and step > 0:
+                src = staged.at[:, :, pl.ds(pl.multiple_of(other * LANES, LANES), LANES)]
+            dst = raw.at[chunk, to, pl.ds(time, count)]
+        arrived = raw_recv.at[lax.rem(jnp.int32(chunk), RAW_SLOTS), to]
+        if step == 0:
+            pltpu.make_async_copy(src, dst, arrived).start()
+        else:
+            pltpu.make_async_remote_copy(
+                src_ref=src, dst_ref=dst, send_sem=raw_send, recv_sem=arrived,
+                device_id=device(link, other), device_id_type=MESH,
+            ).start()
+
+    def spread_rows(*where):
         for step in list(range(1, members)) + [0]:
-            other = lax.rem(member + step, members)
-            lon = pl.multiple_of((to * members + other) * LANES, LANES)
-            if count is None:
-                src = field.at[pl.ds(row, ROWS), pl.ds(lon, LANES)]
-                dst = raw.at[chunk, to, time]
-            else:
-                src = field.at[:, pl.ds(row, ROWS), pl.ds(lon, LANES)]
-                dst = raw.at[chunk, to, pl.ds(time, count)]
-            arrived = raw_recv.at[lax.rem(chunk, RAW_SLOTS), to]
-            if step == 0:
-                pltpu.make_async_copy(src, dst, arrived).start()
-            else:
-                pltpu.make_async_remote_copy(
-                    src_ref=src, dst_ref=dst, send_sem=raw_send, recv_sem=arrived,
-                    device_id=device(link, other), device_id_type=MESH,
-                ).start()
+            spread_one(where[0], where[1], step, *where[2:])
 
     def spread_block(chunk, to):
         if local_rows % lat == 0:
@@ -173,13 +202,16 @@
                 def _():
                     spread_rows(chunk, to, pl.multiple_of(row, ROWS), None, time)
 
-    def each(step, act):
+    def each(step, act, staged_first=False, skip=0):
         for rank in range(CHAIN):
             lag = by_link([ADDED[at][ORDERS[at][rank]] for at in range(CHAIN)])
 
-            @pl.when((step >= lag) & (step < chunks + lag))
+            to = by_link([ORDERS[at][rank] for at in range(CHAIN)])
+            begin = lag + 1 if staged_first and rank == 0 else lag
+
+            @pl.when((step >= begin) & (step < chunks + lag) & ((step >= lag + skip) | ~at_end | (to != inner)))
             def _():
-                act(step - lag, by_link([ORDERS[at][rank] for at in range(CHAIN)]))
+                act(step - lag, to)
 
     spread_steps = chunks + LAST_ADDED
 
@@ -189,7 +221,7 @@
             for away in range(1, members):
                 pl.semaphore_wait(member_free.at[away], 1)
 
-        each(step, spread_block)
+        each(step, spread_block, staged_first=bool(direct), skip=early)
 
     def free_members(step):
         @pl.when(step + RAW_SLOTS < spread_steps)
@@ -234,33 +266,64 @@
             device_id_type=MESH,
         ).start()
 
-    def arrive(chunk, to, up):
+    def take(chunk, to, box):
+        for k in range(SUMS):
+            part[chunk, to, k] = part[chunk, to, k] + box[chunk, to, k]
+
+    def wait_box(chunk, to, up):
         box = below if up else above
         pltpu.make_async_copy(box.at[chunk, to], box.at[chunk, to], box_sem(chunk, to, up, link)).wait()
-        for k in range(SUMS):
-            part[chunk, to, k] = part[chunk, to, k] + box[chunk, to, k]
-
-    def add_up(chunk, to):
-        pltpu.make_async_copy(
-            raw.at[chunk, to], raw.at[chunk, to], raw_recv.at[lax.rem(chunk, RAW_SLOTS), to]
-        ).wait()
+
+    def arrive(chunk, to, up):
+        wait_box(chunk, to, up)
+        take(chunk, to, below if up else above)
+
+    def arrive_own(chunk, up):
+        if early:
+            stands_in = (link == (1 if up else CHAIN - 2)) & (chunk < own_early)
+
+            @pl.when(stands_in)
+            def _():
+                got = early_raw.at[chunk]
+                pltpu.make_async_copy(got, got, early_recv.at[chunk]).wait()
+                sum_span(lambda time: early_raw[chunk, time], inner, below if up else above, chunk, link)
+
+            @pl.when(~stands_in)
+            def _():
+                wait_box(chunk, link, up)
+
+        else:
+            wait_box(chunk, link, up)
+        take(chunk, link, below if up else above)
+
+    def sum_span(value_at, source, result, chunk, to):
+        offset = source.astype(jnp.float32) * np.float32(SPAN / (TIMES / 2.0))
+        quarter = lambda at: (source == at).astype(jnp.float32)
+        turn_cos, turn_sin = quarter(0) - quarter(2), quarter(1) - quarter(3)
+        flip = quarter(0) - quarter(1) + quarter(2) - quarter(3)
         local = [None] * (SLOW + 1)
         whole = None
         for month in range(MONTHS):
             kept = None
             for time in range(month, SPAN, MONTHS):
-                value = raw[chunk, to, time]
+                value = value_at(time)
                 kept = value if kept is None else kept + value
                 terms = [value * np.float32(span[time, k]) for k in range(SLOW)] + [value * value]
                 local = [term if own is None else own + term for own, term in zip(local, terms)]
-            part[chunk, to, month] = kept
+            result[chunk, to, month] = kept
             whole = kept if whole is None else whole + kept
         trend, cosine, sine, double, squares = local
-        part[chunk, to, MONTHS] = trend + whole * offset
-        part[chunk, to, MONTHS + 1] = cosine * turn_cos - sine * turn_sin
-        part[chunk, to, MONTHS + 2] = cosine * turn_sin + sine * turn_cos
-        part[chunk, to, MONTHS + 3] = double * flip
-        part[chunk, to, MONTHS + 4] = squares
+        result[chunk, to, MONTHS] = trend + whole * offset
+        result[chunk, to, MONTHS + 1] = cosine * turn_cos - sine * turn_sin
+        result[chunk, to, MONTHS + 2] = cosine * turn_sin + sine * turn_cos
+        result[chunk, to, MONTHS + 3] = double * flip
+        result[chunk, to, MONTHS + 4] = squares
+
+    def add_up(chunk, to):
+        pltpu.make_async_copy(
+            raw.at[chunk, to], raw.at[chunk, to], raw_recv.at[lax.rem(chunk, RAW_SLOTS), to]
+        ).wait()
+        sum_span(lambda time: raw[chunk, to, time], link, part, chunk, to)
 
         @pl.when((link == 0) & (to > 0))
         def _():
@@ -286,11 +349,11 @@
     def close(chunk):
         @pl.when(link > 0)
         def _():
-            arrive(chunk, link, True)
+            arrive_own(chunk, True)
 
         @pl.when(link < CHAIN - 1)
         def _():
-            arrive(chunk, link, False)
+            arrive_own(chunk, False)
 
         coeffs, variance = finish([part[chunk, link, k] for k in range(SUMS)])
         rows = pl.ds(pl.multiple_of(chunk * ROWS, ROWS), ROWS)
@@ -298,15 +361,78 @@
             coeff_out[k, rows, :] = coeffs[k]
         var_out[rows, :] = variance
 
+    def each_early(act):
+        for chunk in range(early):
+            for away in range(members):
+                other = lax.rem(member + away, members)
+                pl.when(chunk < early_of(other))(functools.partial(act, chunk, away, other))
+
+    def send_early(chunk, away, other):
+        own = early_raw.at[chunk, pl.ds(member * held, held)]
+        pltpu.make_async_remote_copy(
+            src_ref=stage.at[chunk, :, :, pl.ds(pl.multiple_of(other * LANES, LANES), LANES)],
+            dst_ref=passing.at[chunk, away - 1] if away else own,
+            send_sem=raw_send if away else early_send,
+            recv_sem=(passing_recv if away else early_recv).at[chunk],
+            device_id=device(inner, member),
+            device_id_type=MESH,
+        ).start()
+
+    def forward_early(chunk, away, other):
+        if away:
+            pltpu.make_async_remote_copy(
+                src_ref=passing.at[chunk, away - 1],
+                dst_ref=early_raw.at[chunk, pl.ds(member * held, held)],
+                send_sem=early_send,
+                recv_sem=early_recv.at[chunk],
+                device_id=device(link, other),
+                device_id_type=MESH,
+            ).start()
+
+    def wait_passed(sem_of):
+        for chunk in range(early):
+            even, odd = chunk < EARLY_EVEN, chunk < EARLY_ODD
+            for parity in range(2):
+                pieces = members // 2 * (even + odd) - (odd if parity else even)
+
+                @pl.when(lax.rem(member, 2) == parity)
+                def _():
+                    got = passing.at[chunk, pl.ds(0, pieces)]
+                    pltpu.make_async_copy(got, got, sem_of(chunk)).wait()
+
+    def forward():
+        wait_passed(lambda chunk: passing_recv.at[chunk])
+        each_early(forward_early)
+
+    if direct:
+        pltpu.make_async_copy(first_stage, first_stage, stage_sem.at[0]).wait()
+        spread_rows(jnp.int32(0), first_to, 0, held, member * held, first_stage)
+
+        @pl.when(at_end)
+        def _():
+            for chunk in range(early):
+                pltpu.make_async_copy(stage.at[chunk], stage.at[chunk], stage_sem.at[1 + chunk]).wait()
+            each_early(send_early)
+
     lax.fori_loop(0, AHEAD, lambda step, _: (spread(step), 0)[1], 0)
+    if early:
+
+        @pl.when(at_end)
+        def _():
+            for chunk in range(EARLY):
+                for away in range(members):
+                    other = lax.rem(member + away, members)
+                    pl.when(chunk >= early_of(other))(functools.partial(spread_one, chunk, inner, away, chunk * ROWS))
     close_lag = by_link(CLOSE)
 
     def body(step, carry):
         spread(step + AHEAD)
         await_boxes(step)
-        each(step, add_up)
+        each(step, add_up, skip=own_early if early else 0)
         free_members(step)
         relay(step)
+        if early:
+            pl.when((step == FORWARD) & ~at_end)(forward)
 
         @pl.when((step >= close_lag) & (step < chunks + close_lag))
         def _():
@@ -320,8 +446,31 @@
     lons = pl.ds(0, (members - 1) * CHAIN * LANES)
     sent = field.at[:, :, lons] if local_rows % lat == 0 else field.at[:, lons]
     pltpu.make_async_copy(sent, sent, raw_send).wait()
-    passed = part.at[:, pl.ds(0, CHAIN - 1)]
+    passed = part.at[pl.ds(early, chunks - early), pl.ds(0, CHAIN - 1)]
     pltpu.make_async_copy(passed, passed, part_send).wait()
+    if early:
+        passed = part.at[pl.ds(0, early), pl.ds(0, CHAIN - 2)]
+        pltpu.make_async_copy(passed, passed, part_send).wait()
+
+        @pl.when(at_end)
+        def _():
+            for chunk in range(early):
+
+                @pl.when(chunk < own_early)
+                def _():
+                    own = early_raw.at[chunk, pl.ds(0, held)]
+                    pltpu.make_async_copy(own, own, early_send).wait()
+
+                @pl.when(chunk >= own_early)
+                def _():
+                    passed = part.at[chunk, 0]
+                    pltpu.make_async_copy(passed, passed, part_send).wait()
+
+        @pl.when(~at_end)
+        def _():
+            passed = part.at[pl.ds(0, early), 0]
+            pltpu.make_async_copy(passed, passed, part_send).wait()
+            wait_passed(lambda chunk: early_send)
 
 
 def put_out(coeffs, variance, coeff_out, var_out, sem):
@@ -343,7 +492,18 @@
         raise ValueError("unsupported sizes")
     chunks = lat // ROWS
     members = groups // CHAIN
-    field = snapshots.reshape(local_rows // lat, lat, width) if local_rows % lat == 0 else snapshots
+    held, whole = local_rows // lat, local_rows % lat == 0
+    field = snapshots.reshape(held, lat, width) if whole else snapshots
+    direct = [
+        pltpu.VMEM((EARLY, held, ROWS, members * LANES), jnp.float32),
+        pltpu.VMEM((held, ROWS, members * LANES), jnp.float32),
+        pltpu.VMEM((EARLY, members - 1, held, ROWS, LANES), jnp.float32),
+        pltpu.VMEM((EARLY, SPAN, ROWS, LANES), jnp.float32),
+        pltpu.SemaphoreType.DMA((1 + EARLY,)),
+        pltpu.SemaphoreType.DMA((EARLY,)),
+        pltpu.SemaphoreType.DMA((EARLY,)),
+        pltpu.SemaphoreType.DMA,
+    ]
     results = pl.pallas_call(
         functools.partial(kernel, groups, lat, local_rows),
         out_shape=(
@@ -363,6 +523,7 @@
             pltpu.SemaphoreType.DMA((BOX_SLOTS, CHAIN + 1)),
             pltpu.SemaphoreType.REGULAR((members,)),
             pltpu.SemaphoreType.REGULAR((2,)),
+            *(direct if whole else []),
         ],
         compiler_params=pltpu.CompilerParams(
             collective_id=0, has_side_effects=True, vmem_limit_bytes=44 * 2**20

time: 154 us -> 152 us (0.987)
  Pallas kernels: 153 us -> 150 us
    pallas_call x1, Pallas kernels: 152 us -> 149 us  [local(): pl.pallas_call(functools.partial(kernel, groups, lat, local_rows), out_sh...]
where the time goes in v2:
time: 152 us; the launch traced here: 151 us
  Pallas kernels  150 us (99%)
    pallas_call x1, Pallas kernels, local(): pl.pallas_call(functools.partial(kernel, groups, lat, local_rows), out_sh...  149 us

profile of v2, /device:TPU:17, one launch (start us, length us, event | category | flops | bytes accessed | tf_op | source)
XLA Modules:
  0.0 150.6 jit_solution(15176057852111941411)
XLA Ops:
  0.6 148.6 %climatology.1 = (f32[16,256,128]{2,1,0:T(8,128)S(1)}, f32[256,128]{1,0:T(8,128)S(1)}) custom-call(f32[6,256,2048]{2,1,0:T(8,128)} %bitcast.1), custom_call_target="tpu_custom_call" | custom-call | tf_op jit(solution)/shard_map/climatology/pallas_call | solution.py:507
  149.3 1.4 put_out.1

commit v3 on v2

--- a/solution.py
+++ b/solution.py
@@ -26,37 +26,27 @@
 
 
 def schedule():
-    far = [[to for to in sorted(range(CHAIN), key=lambda to: -abs(to - at)) if to != at] for at in range(CHAIN)]
-    orders = [blocks + [at] for at, blocks in enumerate(far)]
-    added = []
+    orders, added = [], []
     for at in range(CHAIN):
-        lags = {}
-        for to in far[at]:
-            side = [other for other in far[at] if (other > at) == (to > at)]
+        far = sorted((to for to in range(CHAIN) if to != at), key=lambda to: -abs(to - at))
+        lags = {at: SKEW * (CHAIN - 2)}
+        for to in far:
+            side = [other for other in far if (other > at) == (to > at)]
             lags[to] = SKEW * side.index(to)
-        lags[at] = SKEW + 1 if at in (0, CHAIN - 1) else SKEW * (CHAIN - 2)
+        orders.append(far + [at])
         added.append(lags)
-    up, down = {}, {}
+    passed, close = {}, []
     for to in range(CHAIN):
-        for at in range(to + 1):
-            up[at, to] = added[0][to] if at == 0 else max(added[at][to], up[at - 1, to] + 1)
-        for at in range(CHAIN - 1, to - 1, -1):
-            down[at, to] = added[at][to] if at == CHAIN - 1 else max(added[at][to], down[at + 1, to] + 1)
-    close = [max(up[at, at], down[at, at]) for at in range(CHAIN)]
-    for at in range(CHAIN):
-        up[at, at] = down[at, at] = close[at]
-    hold = max(
-        [up[at + 1, to] - up[at, to] for at, to in up if at < to]
-        + [down[at - 1, to] - down[at, to] for at, to in down if at > to]
-    )
-    last = max([lag for (at, to), lag in up.items() if at < to] + [lag for (at, to), lag in down.items() if at > to])
-    return orders, added, up, down, close, hold, last
-
-
-ORDERS, ADDED, UP, DOWN, CLOSE, HOLD, LAST_SENT = schedule()
-LAST_ADDED = max(max(lags.values()) for lags in ADDED)
-RAW_SLOTS = AHEAD + 2
-BOX_SLOTS = HOLD + 3
+        for way in (range(to + 1), range(CHAIN - 1, to - 1, -1)):
+            lag = -1
+            for at in way:
+                lag = max(added[at][to], lag + 1)
+                passed[at, to] = max(lag, passed.get((at, to), 0))
+        close.append(passed[to, to])
+    return orders, added, passed, close
+
+
+ORDERS, ADDED, PASSED, CLOSE = schedule()
 
 
 def fit_constants():
@@ -111,16 +101,16 @@
 def kernel(
     groups, lat, local_rows,
     field, coeff_out, var_out,
-    raw, part, below, above,
-    raw_send, raw_recv, part_send, box_recv, member_free, box_free,
-    *direct,
+    raw, part, below, above, direct,
+    raw_send, raw_recv, part_send, box_recv, *direct_sems,
 ):
     members = groups // CHAIN
     chunks = lat // ROWS
     held = local_rows // lat
     early = EARLY if direct else 0
     if direct:
-        stage, first_stage, passing, early_raw, stage_sem, passing_recv, early_recv, early_send = direct
+        stage, first_stage, passing, early_raw = direct
+        stage_sem, passing_recv, early_recv, early_send = direct_sems
     me = lax.axis_index("io")
     link, member = me // members, lax.rem(me, members)
     device = lambda at, who: {"io": at * members + who}
@@ -138,6 +128,19 @@
         lons = pl.ds(pl.multiple_of(to * members * LANES, LANES), members * LANES)
         return field.at[:, pl.ds(chunk * ROWS, ROWS), lons]
 
+    barrier = pltpu.get_barrier_semaphore()
+    @pl.when(link > 0)
+    def _():
+        pl.semaphore_signal(barrier, inc=1, device_id=device(link - 1, member), device_id_type=MESH)
+
+    @pl.when(link < CHAIN - 1)
+    def _():
+        pl.semaphore_signal(barrier, inc=1, device_id=device(link + 1, member), device_id_type=MESH)
+
+    for step in range(1, members):
+        other = lax.rem(member + step, members)
+        pl.semaphore_signal(barrier, inc=1, device_id=device(link, other), device_id_type=MESH)
+
     first_to = by_link([ORDERS[at][0] for at in range(CHAIN)])
     if direct:
         pltpu.make_async_copy(block_of(0, first_to), first_stage, stage_sem.at[0]).start()
@@ -146,19 +149,6 @@
         def _():
             for chunk in range(early):
                 pltpu.make_async_copy(block_of(chunk, inner), stage.at[chunk], stage_sem.at[1 + chunk]).start()
-
-    barrier = pltpu.get_barrier_semaphore()
-    for step in range(1, members):
-        other = lax.rem(member + step, members)
-        pl.semaphore_signal(barrier, inc=1, device_id=device(link, other), device_id_type=MESH)
-
-    @pl.when(link > 0)
-    def _():
-        pl.semaphore_signal(barrier, inc=1, device_id=device(link - 1, member), device_id_type=MESH)
-
-    @pl.when(link < CHAIN - 1)
-    def _():
-        pl.semaphore_signal(barrier, inc=1, device_id=device(link + 1, member), device_id_type=MESH)
 
     ends = (link == 0).astype(jnp.int32) + (link == CHAIN - 1).astype(jnp.int32)
     pl.semaphore_wait(barrier, members + 1 - ends)
@@ -175,7 +165,7 @@
             if staged is not None and step > 0:
                 src = staged.at[:, :, pl.ds(pl.multiple_of(other * LANES, LANES), LANES)]
             dst = raw.at[chunk, to, pl.ds(time, count)]
-        arrived = raw_recv.at[lax.rem(jnp.int32(chunk), RAW_SLOTS), to]
+        arrived = raw_recv.at[chunk, to]
         if step == 0:
             pltpu.make_async_copy(src, dst, arrived).start()
         else:
@@ -213,47 +203,12 @@
             def _():
                 act(step - lag, to)
 
-    spread_steps = chunks + LAST_ADDED
-
     def spread(step):
-        @pl.when((step >= RAW_SLOTS) & (step < spread_steps))
-        def _():
-            for away in range(1, members):
-                pl.semaphore_wait(member_free.at[away], 1)
-
         each(step, spread_block, staged_first=bool(direct), skip=early)
-
-    def free_members(step):
-        @pl.when(step + RAW_SLOTS < spread_steps)
-        def _():
-            for away in range(1, members):
-                other = lax.rem(member + away, members)
-                pl.semaphore_signal(
-                    member_free.at[members - away], inc=1, device_id=device(link, other), device_id_type=MESH
-                )
-
-    send_steps, slack = chunks + LAST_SENT, BOX_SLOTS - HOLD
-
-    def await_boxes(step):
-        for up in (True, False):
-
-            @pl.when((link < CHAIN - 1 if up else link > 0) & (step >= slack) & (step < send_steps))
-            def _():
-                pl.semaphore_wait(box_free.at[0 if up else 1], 1)
-
-    def free_boxes(step):
-        for up in (True, False):
-
-            @pl.when((link > 0 if up else link < CHAIN - 1) & (step + slack < send_steps))
-            def _():
-                pl.semaphore_signal(
-                    box_free.at[0 if up else 1], inc=1,
-                    device_id=device(link - 1 if up else link + 1, member), device_id_type=MESH,
-                )
 
     def box_sem(chunk, to, up, at):
         where = to if up else to + (to == at).astype(jnp.int32) * (CHAIN - to)
-        return box_recv.at[lax.rem(chunk, BOX_SLOTS), where]
+        return box_recv.at[chunk, where]
 
     def send(chunk, to, up):
         at = link + 1 if up else link - 1
@@ -321,7 +276,7 @@
 
     def add_up(chunk, to):
         pltpu.make_async_copy(
-            raw.at[chunk, to], raw.at[chunk, to], raw_recv.at[lax.rem(chunk, RAW_SLOTS), to]
+            raw.at[chunk, to], raw.at[chunk, to], raw_recv.at[chunk, to]
         ).wait()
         sum_span(lambda time: raw[chunk, to, time], link, part, chunk, to)
 
@@ -338,7 +293,7 @@
             for to in range(CHAIN):
                 if to == at:
                     continue
-                lag = UP[at, to] if to > at else DOWN[at, to]
+                lag = PASSED[at, to]
 
                 @pl.when((link == at) & (step >= lag) & (step < chunks + lag))
                 def _():
@@ -427,9 +382,7 @@
 
     def body(step, carry):
         spread(step + AHEAD)
-        await_boxes(step)
         each(step, add_up, skip=own_early if early else 0)
-        free_members(step)
         relay(step)
         if early:
             pl.when((step == FORWARD) & ~at_end)(forward)
@@ -438,10 +391,9 @@
         def _():
             close(step - close_lag)
 
-        free_boxes(step)
         return carry
 
-    lax.fori_loop(0, chunks + max(max(CLOSE), LAST_SENT), body, 0)
+    lax.fori_loop(0, chunks + max(PASSED.values()), body, 0)
 
     lons = pl.ds(0, (members - 1) * CHAIN * LANES)
     sent = field.at[:, :, lons] if local_rows % lat == 0 else field.at[:, lons]
@@ -471,6 +423,29 @@
             passed = part.at[pl.ds(0, early), 0]
             pltpu.make_async_copy(passed, passed, part_send).wait()
             wait_passed(lambda chunk: early_send)
+
+
+def scoped(groups, lat, local_rows, field, coeff_out, var_out, raw, part, below, above, *direct):
+    chunks = lat // ROWS
+    sems = [
+        pltpu.SemaphoreType.DMA,
+        pltpu.SemaphoreType.DMA((chunks, CHAIN)),
+        pltpu.SemaphoreType.DMA,
+        pltpu.SemaphoreType.DMA((chunks, CHAIN + 1)),
+    ]
+    if direct:
+        sems += [
+            pltpu.SemaphoreType.DMA((1 + EARLY,)),
+            pltpu.SemaphoreType.DMA((EARLY,)),
+            pltpu.SemaphoreType.DMA((EARLY,)),
+            pltpu.SemaphoreType.DMA,
+        ]
+    pl.run_scoped(
+        functools.partial(
+            kernel, groups, lat, local_rows, field, coeff_out, var_out, raw, part, below, above, direct
+        ),
+        *sems,
+    )
 
 
 def put_out(coeffs, variance, coeff_out, var_out, sem):
@@ -499,13 +474,9 @@
         pltpu.VMEM((held, ROWS, members * LANES), jnp.float32),
         pltpu.VMEM((EARLY, members - 1, held, ROWS, LANES), jnp.float32),
         pltpu.VMEM((EARLY, SPAN, ROWS, LANES), jnp.float32),
-        pltpu.SemaphoreType.DMA((1 + EARLY,)),
-        pltpu.SemaphoreType.DMA((EARLY,)),
-        pltpu.SemaphoreType.DMA((EARLY,)),
-        pltpu.SemaphoreType.DMA,
     ]
     results = pl.pallas_call(
-        functools.partial(kernel, groups, lat, local_rows),
+        functools.partial(scoped, groups, lat, local_rows),
         out_shape=(
             jax.ShapeDtypeStruct((HARM, lat, LANES), jnp.float32),
             jax.ShapeDtypeStruct((lat, LANES), jnp.float32),
@@ -517,12 +488,6 @@
             pltpu.VMEM((chunks, CHAIN, SUMS, ROWS, LANES), jnp.float32),
             pltpu.VMEM((chunks, CHAIN, SUMS, ROWS, LANES), jnp.float32),
             pltpu.VMEM((chunks, CHAIN, SUMS, ROWS, LANES), jnp.float32),
-            pltpu.SemaphoreType.DMA,
-            pltpu.SemaphoreType.DMA((RAW_SLOTS, CHAIN)),
-            pltpu.SemaphoreType.DMA,
-            pltpu.SemaphoreType.DMA((BOX_SLOTS, CHAIN + 1)),
-            pltpu.SemaphoreType.REGULAR((members,)),
-            pltpu.SemaphoreType.REGULAR((2,)),
             *(direct if whole else []),
         ],
         compiler_params=pltpu.CompilerParams(

time: 152 us -> 151 us (level)
  no operation moved by 1% of the time
where the time goes in v3:
time: 151 us
  Pallas kernels  150 us (99%)
    pallas_call x1, Pallas kernels, local(): pl.pallas_call(functools.partial(scoped, groups, lat, local_rows), out_sh...  149 us

profile of v3, /device:TPU:17, one launch (start us, length us, event | category | flops | bytes accessed | tf_op | source)
XLA Modules:
  0.0 150.6 jit_solution(16914185658019002754)
XLA Ops:
  0.6 148.6 %climatology.1 = (f32[16,256,128]{2,1,0:T(8,128)S(1)}, f32[256,128]{1,0:T(8,128)S(1)}) custom-call(f32[6,256,2048]{2,1,0:T(8,128)} %bitcast.1), custom_call_target="tpu_custom_call" | custom-call | tf_op jit(solution)/shard_map/climatology/pallas_call | solution.py:478
  149.2 1.4 put_out.1

commit v4 on v3

--- a/solution.py
+++ b/solution.py
@@ -361,7 +361,13 @@
 
     if direct:
         pltpu.make_async_copy(first_stage, first_stage, stage_sem.at[0]).wait()
-        spread_rows(jnp.int32(0), first_to, 0, held, member * held, first_stage)
+        for parity in (1, 0):
+            for away in range(1, members):
+                spread_first = functools.partial(
+                    spread_one, jnp.int32(0), first_to, away, 0, held, member * held, first_stage
+                )
+                pl.when(lax.rem(member + away, 2) == parity)(spread_first)
+        spread_one(jnp.int32(0), first_to, 0, 0)
 
         @pl.when(at_end)
         def _():

time: 151 us -> 151 us (level)
  no operation moved by 1% of the time
where the time goes in v4:
time: 151 us
  Pallas kernels  150 us (99%)
    pallas_call x1, Pallas kernels, local(): pl.pallas_call(functools.partial(scoped, groups, lat, local_rows), out_sh...  149 us

profile of v4, /device:TPU:17, one launch (start us, length us, event | category | flops | bytes accessed | tf_op | source)
XLA Modules:
  0.0 150.6 jit_solution(5685514986233924372)
XLA Ops:
  0.6 148.6 %climatology.1 = (f32[16,256,128]{2,1,0:T(8,128)S(1)}, f32[256,128]{1,0:T(8,128)S(1)}) custom-call(f32[6,256,2048]{2,1,0:T(8,128)} %bitcast.1), custom_call_target="tpu_custom_call" | custom-call | tf_op jit(solution)/shard_map/climatology/pallas_call | solution.py:484
  149.2 1.4 put_out.1

commit v5 on v4

--- a/solution.py
+++ b/solution.py
@@ -129,6 +129,10 @@
         return field.at[:, pl.ds(chunk * ROWS, ROWS), lons]
 
     barrier = pltpu.get_barrier_semaphore()
+    for step in range(1, members):
+        other = lax.rem(member + step, members)
+        pl.semaphore_signal(barrier, inc=1, device_id=device(link, other), device_id_type=MESH)
+
     @pl.when(link > 0)
     def _():
         pl.semaphore_signal(barrier, inc=1, device_id=device(link - 1, member), device_id_type=MESH)
@@ -136,10 +140,6 @@
     @pl.when(link < CHAIN - 1)
     def _():
         pl.semaphore_signal(barrier, inc=1, device_id=device(link + 1, member), device_id_type=MESH)
-
-    for step in range(1, members):
-        other = lax.rem(member + step, members)
-        pl.semaphore_signal(barrier, inc=1, device_id=device(link, other), device_id_type=MESH)
 
     first_to = by_link([ORDERS[at][0] for at in range(CHAIN)])
     if direct:
@@ -376,18 +376,19 @@
             each_early(send_early)
 
     lax.fori_loop(0, AHEAD, lambda step, _: (spread(step), 0)[1], 0)
-    if early:
-
-        @pl.when(at_end)
-        def _():
-            for chunk in range(EARLY):
-                for away in range(members):
-                    other = lax.rem(member + away, members)
-                    pl.when(chunk >= early_of(other))(functools.partial(spread_one, chunk, inner, away, chunk * ROWS))
     close_lag = by_link(CLOSE)
 
     def body(step, carry):
         spread(step + AHEAD)
+        if early:
+
+            @pl.when(at_end & (step == SKEW))
+            def _():
+                for chunk in range(EARLY):
+                    for away in range(members):
+                        other = lax.rem(member + away, members)
+                        pl.when(chunk >= early_of(other))(functools.partial(spread_one, chunk, inner, away, chunk * ROWS))
+
         each(step, add_up, skip=own_early if early else 0)
         relay(step)
         if early:

time: 151 us -> 151 us (level)
  no operation moved by 1% of the time
where the time goes in v5:
time: 151 us
  Pallas kernels  150 us (99%)
    pallas_call x1, Pallas kernels, local(): pl.pallas_call(functools.partial(scoped, groups, lat, local_rows), out_sh...  149 us

profile of v5, /device:TPU:17, one launch (start us, length us, event | category | flops | bytes accessed | tf_op | source)
XLA Modules:
  0.0 150.6 jit_solution(11950530129454757117)
XLA Ops:
  0.6 148.6 %climatology.1 = (f32[16,256,128]{2,1,0:T(8,128)S(1)}, f32[256,128]{1,0:T(8,128)S(1)}) custom-call(f32[6,256,2048]{2,1,0:T(8,128)} %bitcast.1), custom_call_target="tpu_custom_call" | custom-call | tf_op jit(solution)/shard_map/climatology/pallas_call | solution.py:485
  149.2 1.4 put_out.1

commit v6 on v5

--- a/solution.py
+++ b/solution.py
@@ -33,7 +33,7 @@
         for to in far:
             side = [other for other in far if (other > at) == (to > at)]
             lags[to] = SKEW * side.index(to)
-        orders.append(far + [at])
+        orders.append(sorted(far, key=lags.get) + [at])
         added.append(lags)
     passed, close = {}, []
     for to in range(CHAIN):

time: 151 us -> 151 us (level)
  no operation moved by 1% of the time
where the time goes in v6:
time: 151 us
  Pallas kernels  150 us (99%)
    pallas_call x1, Pallas kernels, local(): pl.pallas_call(functools.partial(scoped, groups, lat, local_rows), out_sh...  149 us

profile of v6, /device:TPU:17, one launch (start us, length us, event | category | flops | bytes accessed | tf_op | source)
XLA Modules:
  0.0 150.6 jit_solution(17940846216012861330)
XLA Ops:
  0.6 148.6 %climatology.1 = (f32[16,256,128]{2,1,0:T(8,128)S(1)}, f32[256,128]{1,0:T(8,128)S(1)}) custom-call(f32[6,256,2048]{2,1,0:T(8,128)} %bitcast.1), custom_call_target="tpu_custom_call" | custom-call | tf_op jit(solution)/shard_map/climatology/pallas_call | solution.py:485
  149.2 1.4 put_out.1
